TPU v7x, 32 devices: a whole 2x2x4 slice. The times are simulated.
32 devices in a mesh: level: 4 (over z), dev: 8 (over y, x, core).
Axes of the slice: x: 2, y: 2, z: 4, core: 2. Of those that a mesh axis runs over, the one named last changes fastest.
Arguments:
- fields: float32 [4, 128, 12, 128], P('level', 'dev'), may hold values from -6 to 6
- own_src: int32 [4, 128], P('level', 'dev'), may hold values from 0 to 15
- own_weight: bfloat16 [4, 128, 128, 128], P('level', 'dev'), may hold values from 0 to 1, as said below
- send_block: int32 [4, 8, 8, 2], P('level', 'dev'), may hold values from 0 to 15
- send_target: int32 [4, 8, 8, 2], P('level', 'dev'), may hold values from 0 to 15
- send_count: int32 [4, 8, 8], P('level', 'dev'), may hold values from 0 to 2, as said below
- send_weight: bfloat16 [4, 8, 8, 2, 128, 128], P('level', 'dev'), may hold values from 0 to 1, as said below
- left_block: int32 [4, 8, 4, 2], P('level', 'dev'), may hold values from 0 to 15
- left_target: int32 [4, 8, 4, 2], P('level', 'dev'), may hold values from 0 to 15
- left_count: int32 [4, 8, 4], P('level', 'dev'), may hold values from 0 to 2, as said below
- left_weight: bfloat16 [4, 8, 4, 2, 128, 128], P('level', 'dev'), may hold values from 0 to 1, as said below
Outputs:
- remapped: float32 [4, 128, 12, 128], P('level', 'dev')
- totals: float32 [12], replicated
Inputs may be any that keep to these rules, and one draw needn't show every extreme that they name: send_count[l, s, s] = 0; for every level some receiver device gets 2 live slots from every other device of the level. left_count[m, q, m] = 0; for every device index some receiver level gets 2 live slots from every other level. `own_weight`: nonnegative; entry [k, i] is zero where old cell k and new cell i differ by more than 3; each column sums to a positive intersect fraction of at most 1. `send_weight`: nonnegative; entry [k, i] is zero where old cell k and new cell i differ by more than 3; each column sums to a positive intersect fraction of at most 1. `left_weight`: nonnegative; entry [k, i] is zero where old cell k and new cell i differ by more than 3; each column sums to a positive intersect fraction of at most 1.
All inputs are finite; a program needn't handle non-finite values.
Results may differ from a plain program's by a relative error of at most 0.0045.
Values may be sent and summed in bfloat16 or wider, within the bound.
A program may use at most 64 MiB of HBM per device.

v0:
```python
import jax
import jax.numpy as jnp
from jax import lax
from jax.sharding import PartitionSpec as P


def pick_donors(rounded, block_index, count):
    donors = rounded[block_index]
    slots = block_index.shape[1]
    valid = lax.broadcasted_iota(jnp.int32, (1, slots), 1) < count[:, None]
    return jnp.where(valid[:, :, None, None], donors, jnp.zeros_like(donors))


def apply_weights(donors, weights):
    return jnp.einsum("pcmk,pcki->pcmi", donors, weights, preferred_element_type=jnp.float32)


def place_terms(contrib, target, blocks):
    comp = contrib.shape[2]
    cells = contrib.shape[3]
    flat_target = target.reshape(-1)
    onehot = (flat_target[:, None] == lax.broadcasted_iota(jnp.int32, (1, blocks), 1)).astype(
        jnp.float32
    )
    return jnp.einsum(
        "sb,smi->bmi", onehot, contrib.reshape(-1, comp, cells), precision=lax.Precision.HIGHEST
    )


def body(
    fields,
    own_src,
    own_weight,
    send_block,
    send_target,
    send_count,
    send_weight,
    left_block,
    left_target,
    left_count,
    left_weight,
):
    local = fields[0]
    blocks = local.shape[0]
    rounded = local.astype(jnp.bfloat16)
    own = jnp.einsum(
        "bmk,bki->bmi", rounded[own_src[0]], own_weight[0], preferred_element_type=jnp.float32
    )
    donors = pick_donors(rounded, send_block[0, 0], send_count[0, 0])
    strays = pick_donors(rounded, left_block[0, 0], left_count[0, 0])
    intra_terms, intra_target = (
        lax.all_to_all(
            apply_weights(donors, send_weight[0, 0]), "dev", split_axis=0, concat_axis=0, tiled=True
        ),
        lax.all_to_all(send_target[0, 0], "dev", split_axis=0, concat_axis=0, tiled=True),
    )
    left_terms, left_where = (
        lax.all_to_all(
            apply_weights(strays, left_weight[0, 0]),
            "level",
            split_axis=0,
            concat_axis=0,
            tiled=True,
        ),
        lax.all_to_all(left_target[0, 0], "level", split_axis=0, concat_axis=0, tiled=True),
    )
    remapped = (
        own
        + place_terms(intra_terms, intra_target, blocks)
        + place_terms(left_terms, left_where, blocks)
    )
    sums = lax.psum(jnp.sum(remapped, axis=(0, 2)), ("level", "dev"))
    totals = sums / (remapped.shape[2] * blocks)
    return (remapped[None], totals)


def solution(mesh):
    in_specs = (
        P("level", "dev", None, None),
        P("level", "dev"),
        P("level", "dev", None, None),
        P("level", "dev", None, None),
        P("level", "dev", None, None),
        P("level", "dev", None),
        P("level", "dev", None, None, None, None),
        P("level", "dev", None, None),
        P("level", "dev", None, None),
        P("level", "dev", None),
        P("level", "dev", None, None, None, None),
    )
    out_specs = (P("level", "dev", None, None), P())
    return jax.shard_map(body, mesh=mesh, in_specs=in_specs, out_specs=out_specs, check_vma=False)
```

profile of v0, /device:TPU:0, one launch (start us, length us, event | category | flops | bytes accessed | tf_op | source)
XLA Modules:
  0.0 84.1 jit_solution(18198775144529475194)
XLA Ops:
  0.7 0.7 copy-done.3
  1.4 0.6 copy.41
  2.0 6.3 %all-to-all-start.2 = ((s32[4,1,2]{2,1,0:T(1,128)}), s32[4,1,2]{2,1,0:T(1,128)S(1)}, u32[]{:S(2)}, u32[]{:S(2)}) async-start(s32[4,1,2]{2,1,0:T(1,128)} %copy.41), calls=%async_computation.2 | async-start | bytes 4096 | tf_op jit(solution)/shard_map/all_to_all | solution.py:65
  8.4 0.7 fusion.21
  9.0 0.7 iota_compare_fusion.3
  9.8 0.7 compare_select_fusion.1
  10.4 0.7 iota_compare_fusion.2
  11.2 0.7 compare_select_fusion
  12.2 1.3 %copy.36 = s32[8,1,2]{2,1,0:T(1,128)} copy(s32[8,1,2]{0,2,1:T(2,128)} %bitcast.53) | data formatting | bytes 128 | tf_op jit(solution)/shard_map/all_to_all | solution.py:55
  13.6 0.9 %copy.52 = bf16[1,16,12,128]{3,2,1,0:T(8,128)(2,1)S(1)} copy(f32[1,16,12,128]{3,1,2,0:T(8,128)} %param.11) | data formatting | bytes 147456 | tf_op args[0]
  14.5 0.6 gather_fusion.2
  15.1 0.6 gather_fusion.1
  15.6 0.2 fusion.4
  15.9 0.3 fusion.1
  16.2 3.7 %all-to-all-start = ((s32[8,1,2]{2,1,0:T(1,128)}), s32[8,1,2]{2,1,0:T(1,128)S(1)}, u32[]{:S(2)}, u32[]{:S(2)}) async-start(s32[8,1,2]{2,1,0:T(1,128)} %copy.36), calls=%async_computation | async-start | bytes 8192 | tf_op jit(solution)/shard_map/all_to_all | solution.py:55
  19.9 0.6 copy.43
  20.6 4.0 %all-to-all-done = s32[8,1,2]{2,1,0:T(1,128)S(1)} async-done(((s32[8,1,2]{2,1,0:T(1,128)}), s32[8,1,2]{2,1,0:T(1,128)S(1)}, u32[]{:S(2)}, u32[]{:S(2)}) %all-to-all-start) | async-done | bytes 96 | tf_op jit(solution)/shard_map/all_to_all | solution.py:55
  24.5 5.1 %all-to-all-start.3 = ((f32[4,2,12,128]{3,1,2,0:T(2,128)}), f32[4,2,12,128]{3,1,2,0:T(2,128)S(1)}, u32[]{:S(2)}, u32[]{:S(2)}) async-start(f32[4,2,12,128]{3,1,2,0:T(2,128)} %copy.43), calls=%async_computation.3 | async-start | bytes 98304 | tf_op jit(solution)/shard_map/all_to_all | solution.py:58
  29.6 0.6 gather_fusion
  30.2 0.7 copy.38
  30.9 0.5 broadcast.122
  31.4 0.7 reduce.6
  32.2 0.7 reduce.7
  32.9 2.4 %all-to-all-done.3 = f32[4,2,12,128]{3,1,2,0:T(2,128)S(1)} async-done(((f32[4,2,12,128]{3,1,2,0:T(2,128)}), f32[4,2,12,128]{3,1,2,0:T(2,128)S(1)}, u32[]{:S(2)}, u32[]{:S(2)}) %all-to-all-start.3) | async-done | bytes 49184 | tf_op jit(solution)/shard_map/all_to_all | solution.py:58
  35.3 3.4 %all-to-all-start.1 = ((f32[8,2,12,128]{3,1,2,0:T(2,128)}), f32[8,2,12,128]{3,1,2,0:T(2,128)S(1)}, u32[]{:S(2)}, u32[]{:S(2)}) async-start(f32[8,2,12,128]{3,1,2,0:T(2,128)} %copy.38), calls=%async_computation.1 | async-start | bytes 196608 | tf_op jit(solution)/shard_map/all_to_all | solution.py:52
  38.7 0.3 fusion.18
  39.0 4.8 %all-to-all-done.1 = f32[8,2,12,128]{3,1,2,0:T(2,128)S(1)} async-done(((f32[8,2,12,128]{3,1,2,0:T(2,128)}), f32[8,2,12,128]{3,1,2,0:T(2,128)S(1)}, u32[]{:S(2)}, u32[]{:S(2)}) %all-to-all-start.1) | async-done | bytes 98336 | tf_op jit(solution)/shard_map/all_to_all | solution.py:52
  43.9 0.2 fusion.14
  44.1 0.4 fusion.24
  44.4 38.5 %psum.7 = f32[12]{0:T(128)S(1)} all-reduce(f32[12]{0:T(128)S(1)} %get-tuple-element.8), channel_id=1, replica_groups=mesh['level'=4,'dev'=8] {'level','dev'}, use_global_device_ids=true, to_apply=%region_1.2 | all-reduce | flops 12 | bytes 96 | tf_op jit(solution)/shard_map/psum | solution.py:72
  82.9 0.5 broadcast_multiply_fusion
  83.4 0.7 copy.46
  (19 shorter events, 0.6 us)
Async XLA Ops:
  0.6 43.4 %copy-start = (bf16[1,16,128,128]{3,2,1,0:T(8,128)(2,1)S(1)}, bf16[1,16,128,128]{3,2,1,0:T(8,128)(2,1)}, u32[]{:S(2)}) copy-start(bf16[1,16,128,128]{3,2,1,0:T(8,128)(2,1)} %param.13) | copy-start | bytes 1572868
  0.6 0.7 copy-start.3
  0.7 15.0 %copy-start.2 = (bf16[1,1,4,2,128,128]{5,4,3,2,1,0:T(8,128)(2,1)S(1)}, bf16[1,1,4,2,128,128]{5,4,3,2,1,0:T(8,128)(2,1)}, u32[]{:S(2)}) copy-start(bf16[1,1,4,2,128,128]{5,4,3,2,1,0:T(8,128)(2,1)} %param.21) | copy-start | bytes 786436
  0.7 15.2 %copy-start.1 = (bf16[1,1,8,2,128,128]{5,4,3,2,1,0:T(8,128)(2,1)S(1)}, bf16[1,1,8,2,128,128]{5,4,3,2,1,0:T(8,128)(2,1)}, u32[]{:S(2)}) copy-start(bf16[1,1,8,2,128,128]{5,4,3,2,1,0:T(8,128)(2,1)} %param.17) | copy-start | bytes 1572868
  2.0 14.2 %all-to-all-start.2 = ((s32[4,1,2]{2,1,0:T(1,128)}), s32[4,1,2]{2,1,0:T(1,128)S(1)}, u32[]{:S(2)}, u32[]{:S(2)}) async-start(s32[4,1,2]{2,1,0:T(1,128)} %copy.41), calls=%async_computation.2 | async-start | bytes 4096 | tf_op jit(solution)/shard_map/all_to_all | solution.py:65
  16.2 8.3 %all-to-all-start = ((s32[8,1,2]{2,1,0:T(1,128)}), s32[8,1,2]{2,1,0:T(1,128)S(1)}, u32[]{:S(2)}, u32[]{:S(2)}) async-start(s32[8,1,2]{2,1,0:T(1,128)} %copy.36), calls=%async_computation | async-start | bytes 8192 | tf_op jit(solution)/shard_map/all_to_all | solution.py:55
  24.5 10.8 %all-to-all-start.3 = ((f32[4,2,12,128]{3,1,2,0:T(2,128)}), f32[4,2,12,128]{3,1,2,0:T(2,128)S(1)}, u32[]{:S(2)}, u32[]{:S(2)}) async-start(f32[4,2,12,128]{3,1,2,0:T(2,128)} %copy.43), calls=%async_computation.3 | async-start | bytes 98304 | tf_op jit(solution)/shard_map/all_to_all | solution.py:58
  35.3 8.5 %all-to-all-start.1 = ((f32[8,2,12,128]{3,1,2,0:T(2,128)}), f32[8,2,12,128]{3,1,2,0:T(2,128)S(1)}, u32[]{:S(2)}, u32[]{:S(2)}) async-start(f32[8,2,12,128]{3,1,2,0:T(2,128)} %copy.38), calls=%async_computation.1 | async-start | bytes 196608 | tf_op jit(solution)/shard_map/all_to_all | solution.py:52
where the time goes:
time: 84.7 us; the launch traced here: 84.1 us
  blocking collectives  38.5 us (45%)
  starting transfers between devices  18.5 us (22%)
  waiting for transfers between devices  11.2 us (13%)
  local copies, waits for them, and re-layouts  8.43 us (10%)
  other arithmetic  5.33 us (6%)
  matrix products  1.38 us (2%)
    psum x1, blocking collectives, body(): sums = lax.psum(jnp.sum(remapped, axis=(0, 2)), ('level', 'dev'))  38.5 us
    all_to_all x1, starting transfers between devices, body(): lax.all_to_all(left_target[0, 0], 'level', split_axis=0, concat_axis=0, t...  6.35 us
    all_to_all x1, starting transfers between devices, body(): lax.all_to_all(apply_weights(strays, left_weight[0, 0]), 'level', split_a...  5.09 us
    all_to_all x1, waiting for transfers between devices, body(): lax.all_to_all(apply_weights(donors, send_weight[0, 0]), 'dev', split_axi...  4.79 us
    all_to_all x1, waiting for transfers between devices, body(): lax.all_to_all(send_target[0, 0], 'dev', split_axis=0, concat_axis=0, til...  3.97 us
    all_to_all x1, starting transfers between devices, body(): lax.all_to_all(send_target[0, 0], 'dev', split_axis=0, concat_axis=0, til...  3.74 us
    all_to_all x1, starting transfers between devices, body(): lax.all_to_all(apply_weights(donors, send_weight[0, 0]), 'dev', split_axi...  3.36 us
    all_to_all x1, waiting for transfers between devices, body(): lax.all_to_all(apply_weights(strays, left_weight[0, 0]), 'level', split_a...  2.42 us
  transfers between devices with their start and end apart: 4, of which 3 were waited for; matrix products, arithmetic and copies ran while one was open for 14% of the time, Pallas kernels for 0%

commit v1 on v0

v1 whole, which is shorter than its diff:
```python
import functools

import jax
import jax.numpy as jnp
from jax import lax
from jax.experimental import pallas as pl
from jax.experimental.pallas import tpu as pltpu
from jax.sharding import PartitionSpec as P

MESH = pl.DeviceIdType.MESH
F32 = jnp.float32
BF16 = jnp.bfloat16


def kernel(
    nd,
    nl,
    own_src,
    send_block,
    send_target,
    send_count,
    left_block,
    left_target,
    left_count,
    fields_hbm,
    own_hbm,
    send_hbm,
    left_hbm,
    out_ref,
    tot_ref,
    fields,
    own_w,
    send_w,
    left_w,
    load_sem,
    sbuf,
    rbuf,
    s_sem,
    r_sem,
    lsbuf,
    lrbuf,
    ls_sem,
    lr_sem,
    tbuf,
    trecv,
    ts_sem,
    tr_sem,
    ubuf,
    urecv,
    us_sem,
    ur_sem,
):
    dev = lax.axis_index("dev")
    lvl = lax.axis_index("level")
    blocks, cells = own_w.shape[:2]
    comp = fields.shape[0] // blocks
    cap = send_w.shape[1]
    lcap = left_w.shape[1]
    rows = sbuf.shape[1] // cap

    loads = [
        pltpu.make_async_copy(src, dst, load_sem.at[i])
        for i, (src, dst) in enumerate(
            ((fields_hbm, fields), (left_hbm, left_w), (send_hbm, send_w), (own_hbm, own_w))
        )
    ]
    for load in loads:
        load.start()

    def dev_peer(r):
        return {"dev": lax.rem(dev + r, nd)}

    def lvl_peer(r):
        return {"level": lax.rem(lvl + r, nl)}

    barrier = pltpu.get_barrier_semaphore()
    for r in range(1, nd):
        pl.semaphore_signal(barrier, inc=1, device_id=dev_peer(r), device_id_type=MESH)
    for r in range(1, nl):
        pl.semaphore_signal(barrier, inc=1, device_id=lvl_peer(r), device_id_type=MESH)

    part = jnp.zeros((comp, cells), F32)

    def donor(index):
        return fields[pl.ds(index, comp, stride=blocks), :]

    def product(block, weight):
        return jnp.dot(block.astype(BF16), weight, preferred_element_type=F32)

    def message(buf, r, c, slot_block, slot_target, slot_count, weights, peer):
        block = donor(slot_block[c, peer])
        block = jnp.where(c < slot_count[0, peer], block, jnp.zeros_like(block))
        term = product(block, weights[peer, c])
        target = jnp.full((rows - comp, cells), slot_target[c, peer].astype(F32), F32)
        buf[r, c * rows : (c + 1) * rows, :] = jnp.concatenate([term, target], axis=0).astype(BF16)
        return term

    loads[0].wait()
    loads[1].wait()
    for r in range(1, nl):
        peer = lax.rem(lvl + r, nl)
        for c in range(lcap):
            part += message(lsbuf, r, c, left_block, left_target, left_count, left_w, peer)
    loads[2].wait()
    for r in range(1, nd):
        peer = lax.rem(dev + r, nd)
        for c in range(cap):
            part += message(sbuf, r, c, send_block, send_target, send_count, send_w, peer)

    pl.semaphore_wait(barrier, nd - 1 + nl - 1)

    sends = []

    def send(src, dst, s, d, who):
        copy = pltpu.make_async_remote_copy(
            src_ref=src, dst_ref=dst, send_sem=s, recv_sem=d, device_id=who, device_id_type=MESH
        )
        copy.start()
        sends.append(copy)
        return copy

    lefts = [
        send(lsbuf.at[r], lrbuf.at[r], ls_sem.at[r], lr_sem.at[r], lvl_peer(r))
        for r in range(1, nl)
    ]
    intras = [
        send(sbuf.at[r], rbuf.at[r], s_sem.at[r], r_sem.at[r], dev_peer(r)) for r in range(1, nd)
    ]

    loads[3].wait()
    acc = []
    for b in range(blocks):
        term = product(donor(own_src[0, b]), own_w[b])
        part += term
        acc.append(term)

    sums = jnp.sum(part, axis=1, keepdims=True)
    same = lax.broadcasted_iota(jnp.int32, (comp, cells), 0) == lax.broadcasted_iota(
        jnp.int32, (comp, cells), 1
    )
    row = jnp.sum(jnp.where(same, sums, 0.0), axis=0, keepdims=True)
    tbuf[...] = row
    tots = [
        send(tbuf, trecv.at[r], ts_sem.at[r], tr_sem.at[r], dev_peer(r)) for r in range(1, nd)
    ]
    for r, copy in enumerate(tots, 1):
        copy.wait_recv()
        row += trecv[r]
    ubuf[...] = row
    tops = [
        send(ubuf, urecv.at[r], us_sem.at[r], ur_sem.at[r], lvl_peer(r)) for r in range(1, nl)
    ]

    def place(buf, r, slots):
        for c in range(slots):
            got = buf[r, c * rows : (c + 1) * rows, :].astype(F32)
            term = got[:comp]
            target = jnp.broadcast_to(got[comp : comp + 1], (comp, cells))
            for b in range(blocks):
                acc[b] = acc[b] + jnp.where(target == float(b), term, 0.0)

    for r, copy in enumerate(intras, 1):
        copy.wait_recv()
        place(rbuf, r, cap)
    for r, copy in enumerate(lefts, 1):
        copy.wait_recv()
        place(lrbuf, r, lcap)
    for b in range(blocks):
        out_ref[pl.ds(b, comp, stride=blocks), :] = acc[b]
    for r, copy in enumerate(tops, 1):
        copy.wait_recv()
        row += urecv[r]
    tot_ref[...] = (row / (cells * blocks))[0, :comp]
    for copy in sends:
        copy.wait_send()


def solution(mesh):
    nd = mesh.shape["dev"]
    nl = mesh.shape["level"]

    def body(
        fields,
        own_src,
        own_weight,
        send_block,
        send_target,
        send_count,
        send_weight,
        left_block,
        left_target,
        left_count,
        left_weight,
    ):
        blocks, comp, cells = fields.shape[1:]
        cap = send_weight.shape[3]
        lcap = left_weight.shape[3]
        rows = -(-(comp + 1) // 16) * 16
        smem = pl.BlockSpec(memory_space=pltpu.SMEM)
        hbm = pl.BlockSpec(memory_space=pl.ANY)
        vmem = pl.BlockSpec(memory_space=pltpu.VMEM)
        dma = pltpu.SemaphoreType.DMA
        remapped, totals = pl.pallas_call(
            functools.partial(kernel, nd, nl),
            out_shape=(
                jax.ShapeDtypeStruct((comp * blocks, cells), F32),
                jax.ShapeDtypeStruct((comp,), F32),
            ),
            in_specs=[smem] * 7 + [hbm] * 4,
            out_specs=(vmem, vmem),
            scratch_shapes=[
                pltpu.VMEM((comp * blocks, cells), F32),
                pltpu.VMEM((blocks, cells, cells), BF16),
                pltpu.VMEM((nd, cap, cells, cells), BF16),
                pltpu.VMEM((nl, lcap, cells, cells), BF16),
                dma((4,)),
                pltpu.VMEM((nd, cap * rows, cells), BF16),
                pltpu.VMEM((nd, cap * rows, cells), BF16),
                dma((nd,)),
                dma((nd,)),
                pltpu.VMEM((nl, lcap * rows, cells), BF16),
                pltpu.VMEM((nl, lcap * rows, cells), BF16),
                dma((nl,)),
                dma((nl,)),
                pltpu.VMEM((1, cells), F32),
                pltpu.VMEM((nd, 1, cells), F32),
                dma((nd,)),
                dma((nd,)),
                pltpu.VMEM((1, cells), F32),
                pltpu.VMEM((nl, 1, cells), F32),
                dma((nl,)),
                dma((nl,)),
            ],
            compiler_params=pltpu.CompilerParams(collective_id=0, has_side_effects=True),
        )(
            own_src,
            send_block[0, 0].T,
            send_target[0, 0].T,
            send_count[0],
            left_block[0, 0].T,
            left_target[0, 0].T,
            left_count[0],
            fields[0].transpose(1, 0, 2).reshape(comp * blocks, cells),
            own_weight[0],
            send_weight[0, 0],
            left_weight[0, 0],
        )
        remapped = remapped.reshape(comp, blocks, cells).transpose(1, 0, 2)
        return remapped[None], totals

    in_specs = (
        P("level", "dev", None, None),
        P("level", "dev"),
        P("level", "dev", None, None),
        P("level", "dev", None, None),
        P("level", "dev", None, None),
        P("level", "dev", None),
        P("level", "dev", None, None, None, None),
        P("level", "dev", None, None),
        P("level", "dev", None, None),
        P("level", "dev", None),
        P("level", "dev", None, None, None, None),
    )
    out_specs = (P("level", "dev", None, None), P())
    return jax.shard_map(body, mesh=mesh, in_specs=in_specs, out_specs=out_specs, check_vma=False)
```

time: 84.7 us -> 17.2 us (0.20)
  blocking collectives: 38.5 us -> 0 us
  starting transfers between devices: 18.5 us -> 0 us
  Pallas kernels: 0 us -> 14.3 us
  waiting for transfers between devices: 11.2 us -> 0 us
  local copies, waits for them, and re-layouts: 8.43 us -> 2.06 us
  other arithmetic: 5.33 us -> 0 us
  matrix products: 1.38 us -> 0 us
    psum x1 -> x0, blocking collectives: 38.5 us -> none  [body(): sums = lax.psum(jnp.sum(remapped, axis=(0, 2)), ('level', 'dev'))]
    all_to_all x4 -> x0, starting transfers between devices: 18.5 us -> none  [the longest x1 6.35 us: body(): lax.all_to_all(left_target[0, 0], 'level', split_axis=0, concat_axis=0, t...]
    pallas_call x0 -> x1, Pallas kernels: none -> 14.3 us  [body(): pl.pallas_call(functools.partial(kernel, nd, nl), out_shape=(jax.ShapeDty...]
    all_to_all x4 -> x0, waiting for transfers between devices: 11.2 us -> none  [the longest x1 4.79 us: body(): lax.all_to_all(apply_weights(donors, send_weight[0, 0]), 'dev', split_axi...]
    all_to_all x5 -> x0, local copies, waits for them, and re-layouts: 2.56 us -> none  [the longest x1 1.35 us: body(): lax.all_to_all(send_target[0, 0], 'dev', split_axis=0, concat_axis=0, til...]
    select_n x3 -> x0, other arithmetic: 2.02 us -> none  [the longest x2 1.36 us: pick_donors(): donors = rounded[block_index]]
    gather x3 -> x0, local copies, waits for them, and re-layouts: 1.71 us -> none  [the longest x2 1.14 us: pick_donors(): donors = rounded[block_index]]
    lt x2 -> x0, other arithmetic: 1.45 us -> none  [pick_donors(): valid = lax.broadcasted_iota(jnp.int32, (1, slots), 1) < count[:, None]]
  transfers between devices with their start and end apart: 4 -> 0, of which waited for: 3 -> 0; matrix products, arithmetic and copies ran while one was open for 14% -> 0% of each run, Pallas kernels for 0% -> 0%
where the time goes in v1:
time: 17.2 us; the launch traced here: 17 us
  Pallas kernels  14.3 us (83%)
  local copies, waits for them, and re-layouts  2.06 us (12%)
  between operations  0.65 us (4%)
    pallas_call x1, Pallas kernels, body(): pl.pallas_call(functools.partial(kernel, nd, nl), out_shape=(jax.ShapeDty...  14.3 us
    unnamed x4, local copies, waits for them, and re-layouts  2.06 us

profile of v1, /device:TPU:0, one launch (start us, length us, event | category | flops | bytes accessed | tf_op | source)
XLA Modules:
  0.0 17.0 jit_solution(9749258186671212391)
XLA Ops:
  0.6 14.3 %shard_map.122 = (f32[192,128]{1,0:T(8,128)}, f32[12]{0:T(128)}) custom-call(s32[1,16]{1,0:T(1,128)} %own_src.1, s32[2,8]{1,0:T(2,128)} %bitcast.32, s32[2,8]{1,0:T(2,128)} %bitcast.33, s32[1,8]{1,0:T(1,128)} %bitcast.36, s32[2,4]{1,0:T(2,128)} %bitcast.34, s32[2,4]{1,0:T(2,128)} %bitcast.35, s32[1,4]{1,0:T(1,128)} %bitcast.37, f32[192,128]{1,0:T(8,128)} %bitcast.30, ...), custom_call_target="tpu_custom_call" | custom-call | tf_op jit(solution)/shard_map/pallas_call | solution.py:203
  14.9 0.0 copy-start
  15.0 1.5 %copy.15 = f32[1,16,12,128]{3,1,2,0:T(8,128)} copy(f32[1,16,12,128]{3,1,2,0:T(8,128)} %bitcast.31) | data formatting | bytes 196608
  16.5 0.0 copy-done
  16.5 0.5 %copy.16 = f32[12]{0:T(128)} copy(f32[12]{0:T(128)S(1)} %copy-done) | data formatting | bytes 96
Async XLA Ops:
  14.9 1.6 %copy-start = (f32[12]{0:T(128)S(1)}, f32[12]{0:T(128)}, u32[]{:S(2)}) copy-start(f32[12]{0:T(128)} %get-tuple-element.9) | copy-start | bytes 148

commit v2 on v1

--- a/solution.py
+++ b/solution.py
@@ -15,6 +15,19 @@
 def kernel(
     nd,
     nl,
+    own_src_hbm,
+    send_block_hbm,
+    send_target_hbm,
+    send_count_hbm,
+    left_block_hbm,
+    left_target_hbm,
+    left_count_hbm,
+    fields_hbm,
+    own_hbm,
+    send_hbm,
+    left_hbm,
+    out_ref,
+    tot_ref,
     own_src,
     send_block,
     send_target,
@@ -22,12 +35,6 @@
     left_block,
     left_target,
     left_count,
-    fields_hbm,
-    own_hbm,
-    send_hbm,
-    left_hbm,
-    out_ref,
-    tot_ref,
     fields,
     own_w,
     send_w,
@@ -58,15 +65,6 @@
     lcap = left_w.shape[1]
     rows = sbuf.shape[1] // cap
 
-    loads = [
-        pltpu.make_async_copy(src, dst, load_sem.at[i])
-        for i, (src, dst) in enumerate(
-            ((fields_hbm, fields), (left_hbm, left_w), (send_hbm, send_w), (own_hbm, own_w))
-        )
-    ]
-    for load in loads:
-        load.start()
-
     def dev_peer(r):
         return {"dev": lax.rem(dev + r, nd)}
 
@@ -78,6 +76,25 @@
         pl.semaphore_signal(barrier, inc=1, device_id=dev_peer(r), device_id_type=MESH)
     for r in range(1, nl):
         pl.semaphore_signal(barrier, inc=1, device_id=lvl_peer(r), device_id_type=MESH)
+
+    pairs = (
+        (left_block_hbm, left_block),
+        (left_target_hbm, left_target),
+        (left_count_hbm, left_count),
+        (fields_hbm, fields),
+        (left_hbm, left_w),
+        (send_block_hbm, send_block),
+        (send_target_hbm, send_target),
+        (send_count_hbm, send_count),
+        (send_hbm, send_w),
+        (own_src_hbm, own_src),
+        (own_hbm, own_w),
+    )
+    loads = [
+        pltpu.make_async_copy(src, dst, load_sem.at[i]) for i, (src, dst) in enumerate(pairs)
+    ]
+    for load in loads:
+        load.start()
 
     part = jnp.zeros((comp, cells), F32)
 
@@ -95,13 +112,14 @@
         buf[r, c * rows : (c + 1) * rows, :] = jnp.concatenate([term, target], axis=0).astype(BF16)
         return term
 
-    loads[0].wait()
-    loads[1].wait()
+    for load in loads[:5]:
+        load.wait()
     for r in range(1, nl):
         peer = lax.rem(lvl + r, nl)
         for c in range(lcap):
             part += message(lsbuf, r, c, left_block, left_target, left_count, left_w, peer)
-    loads[2].wait()
+    for load in loads[5:9]:
+        load.wait()
     for r in range(1, nd):
         peer = lax.rem(dev + r, nd)
         for c in range(cap):
@@ -127,7 +145,8 @@
         send(sbuf.at[r], rbuf.at[r], s_sem.at[r], r_sem.at[r], dev_peer(r)) for r in range(1, nd)
     ]
 
-    loads[3].wait()
+    for load in loads[9:]:
+        load.wait()
     acc = []
     for b in range(blocks):
         term = product(donor(own_src[0, b]), own_w[b])
@@ -196,24 +215,31 @@
         cap = send_weight.shape[3]
         lcap = left_weight.shape[3]
         rows = -(-(comp + 1) // 16) * 16
-        smem = pl.BlockSpec(memory_space=pltpu.SMEM)
+        smem = functools.partial(pltpu.SMEM, dtype=jnp.int32)
         hbm = pl.BlockSpec(memory_space=pl.ANY)
         vmem = pl.BlockSpec(memory_space=pltpu.VMEM)
         dma = pltpu.SemaphoreType.DMA
         remapped, totals = pl.pallas_call(
             functools.partial(kernel, nd, nl),
             out_shape=(
-                jax.ShapeDtypeStruct((comp * blocks, cells), F32),
-                jax.ShapeDtypeStruct((comp,), F32),
+                pltpu.VMEM((comp * blocks, cells), F32),
+                pltpu.VMEM((comp,), F32),
             ),
-            in_specs=[smem] * 7 + [hbm] * 4,
+            in_specs=[hbm] * 11,
             out_specs=(vmem, vmem),
             scratch_shapes=[
+                smem((1, blocks)),
+                smem((cap, nd)),
+                smem((cap, nd)),
+                smem((1, nd)),
+                smem((lcap, nl)),
+                smem((lcap, nl)),
+                smem((1, nl)),
                 pltpu.VMEM((comp * blocks, cells), F32),
                 pltpu.VMEM((blocks, cells, cells), BF16),
                 pltpu.VMEM((nd, cap, cells, cells), BF16),
                 pltpu.VMEM((nl, lcap, cells, cells), BF16),
-                dma((4,)),
+                dma((11,)),
                 pltpu.VMEM((nd, cap * rows, cells), BF16),
                 pltpu.VMEM((nd, cap * rows, cells), BF16),
                 dma((nd,)),

time: 17.2 us -> 15 us (0.87)
  Pallas kernels: 14.3 us -> 13.1 us
  local copies, waits for them, and re-layouts: 2.06 us -> 1.15 us
    pallas_call x1, Pallas kernels: 14.3 us -> 13.1 us  [body(): pl.pallas_call(functools.partial(kernel, nd, nl), out_shape=(pltpu.VMEM((...]
    unnamed x4 -> x2, local copies, waits for them, and re-layouts: 2.06 us -> 1.15 us
where the time goes in v2:
time: 15 us; the launch traced here: 14.9 us
  Pallas kernels  13.1 us (87%)
  local copies, waits for them, and re-layouts  1.15 us (8%)
  between operations  0.64 us (4%)
    pallas_call x1, Pallas kernels, body(): pl.pallas_call(functools.partial(kernel, nd, nl), out_shape=(pltpu.VMEM((...  13.1 us
    unnamed x2, local copies, waits for them, and re-layouts  1.15 us

profile of v2, /device:TPU:0, one launch (start us, length us, event | category | flops | bytes accessed | tf_op | source)
XLA Modules:
  0.0 14.9 jit_solution(17134660439334882376)
XLA Ops:
  0.6 13.1 %shard_map.122 = (f32[192,128]{1,0:T(8,128)S(1)}, f32[12]{0:T(128)S(1)}) custom-call(s32[1,16]{1,0:T(1,128)} %own_src_hbm.1, s32[2,8]{1,0:T(2,128)} %bitcast.32, s32[2,8]{1,0:T(2,128)} %bitcast.33, s32[1,8]{1,0:T(1,128)} %bitcast.36, s32[2,4]{1,0:T(2,128)} %bitcast.34, s32[2,4]{1,0:T(2,128)} %bitcast.35, s32[1,4]{1,0:T(1,128)} %bitcast.37, ...), custom_call_target="tpu_custom_call" | custom-call | tf_op jit(solution)/shard_map/pallas_call | solution.py:222
  13.7 0.6 %copy.15 = f32[1,16,12,128]{3,1,2,0:T(8,128)} copy(f32[1,16,12,128]{3,1,2,0:T(8,128)S(1)} %bitcast.27) | data formatting | bytes 196608
  14.4 0.5 %copy.16 = f32[12]{0:T(128)} copy(f32[12]{0:T(128)S(1)} %get-tuple-element.7) | data formatting | bytes 96

commit v3 on v2

--- a/solution.py
+++ b/solution.py
@@ -15,6 +15,7 @@
 def kernel(
     nd,
     nl,
+    direct,
     own_src_hbm,
     send_block_hbm,
     send_target_hbm,
@@ -65,28 +66,31 @@
     lcap = left_w.shape[1]
     rows = sbuf.shape[1] // cap
 
-    def dev_peer(r):
-        return {"dev": lax.rem(dev + r, nd)}
-
-    def lvl_peer(r):
-        return {"level": lax.rem(lvl + r, nl)}
-
     barrier = pltpu.get_barrier_semaphore()
-    for r in range(1, nd):
-        pl.semaphore_signal(barrier, inc=1, device_id=dev_peer(r), device_id_type=MESH)
-    for r in range(1, nl):
-        pl.semaphore_signal(barrier, inc=1, device_id=lvl_peer(r), device_id_type=MESH)
-
+    def peer_of(l, r):
+        return {"level": lax.rem(lvl + l, nl), "dev": lax.rem(dev + r, nd)}
+
+    offsets = [
+        (l, r)
+        for l in range(nl)
+        for r in range(nd)
+        if (l or r) and (direct or not (l and r))
+    ]
+    for l, r in offsets:
+        pl.semaphore_signal(barrier, inc=1, device_id=peer_of(l, r), device_id_type=MESH)
+
+    left_peers = [lax.rem(lvl + r, nl) for r in range(1, nl)]
+    send_peers = [lax.rem(dev + r, nd) for r in range(1, nd)]
     pairs = (
         (left_block_hbm, left_block),
         (left_target_hbm, left_target),
         (left_count_hbm, left_count),
         (fields_hbm, fields),
-        (left_hbm, left_w),
+        *[(left_hbm.at[p], left_w.at[p]) for p in left_peers],
         (send_block_hbm, send_block),
         (send_target_hbm, send_target),
         (send_count_hbm, send_count),
-        (send_hbm, send_w),
+        *[(send_hbm.at[p], send_w.at[p]) for p in send_peers],
         (own_src_hbm, own_src),
         (own_hbm, own_w),
     )
@@ -112,20 +116,22 @@
         buf[r, c * rows : (c + 1) * rows, :] = jnp.concatenate([term, target], axis=0).astype(BF16)
         return term
 
-    for load in loads[:5]:
+    first = 4 + len(left_peers)
+    second = first + 3 + len(send_peers)
+    for load in loads[:first]:
         load.wait()
     for r in range(1, nl):
         peer = lax.rem(lvl + r, nl)
         for c in range(lcap):
             part += message(lsbuf, r, c, left_block, left_target, left_count, left_w, peer)
-    for load in loads[5:9]:
+    for load in loads[first:second]:
         load.wait()
     for r in range(1, nd):
         peer = lax.rem(dev + r, nd)
         for c in range(cap):
             part += message(sbuf, r, c, send_block, send_target, send_count, send_w, peer)
 
-    pl.semaphore_wait(barrier, nd - 1 + nl - 1)
+    pl.semaphore_wait(barrier, len(offsets))
 
     sends = []
 
@@ -138,14 +144,14 @@
         return copy
 
     lefts = [
-        send(lsbuf.at[r], lrbuf.at[r], ls_sem.at[r], lr_sem.at[r], lvl_peer(r))
+        send(lsbuf.at[r], lrbuf.at[r], ls_sem.at[r], lr_sem.at[r], peer_of(r, 0))
         for r in range(1, nl)
     ]
     intras = [
-        send(sbuf.at[r], rbuf.at[r], s_sem.at[r], r_sem.at[r], dev_peer(r)) for r in range(1, nd)
+        send(sbuf.at[r], rbuf.at[r], s_sem.at[r], r_sem.at[r], peer_of(0, r)) for r in range(1, nd)
     ]
 
-    for load in loads[9:]:
+    for load in loads[second:]:
         load.wait()
     acc = []
     for b in range(blocks):
@@ -159,16 +165,24 @@
     )
     row = jnp.sum(jnp.where(same, sums, 0.0), axis=0, keepdims=True)
     tbuf[...] = row
-    tots = [
-        send(tbuf, trecv.at[r], ts_sem.at[r], tr_sem.at[r], dev_peer(r)) for r in range(1, nd)
-    ]
-    for r, copy in enumerate(tots, 1):
-        copy.wait_recv()
-        row += trecv[r]
-    ubuf[...] = row
-    tops = [
-        send(ubuf, urecv.at[r], us_sem.at[r], ur_sem.at[r], lvl_peer(r)) for r in range(1, nl)
-    ]
+    if direct:
+        tops = [
+            send(tbuf, urecv.at[i], us_sem.at[i], ur_sem.at[i], peer_of(l, r))
+            for i, (l, r) in enumerate(offsets)
+        ]
+    else:
+        tots = [
+            send(tbuf, trecv.at[r], ts_sem.at[r], tr_sem.at[r], peer_of(0, r))
+            for r in range(1, nd)
+        ]
+        for r, copy in enumerate(tots, 1):
+            copy.wait_recv()
+            row += trecv[r]
+        ubuf[...] = row
+        tops = [
+            send(ubuf, urecv.at[i], us_sem.at[i], ur_sem.at[i], peer_of(i + 1, 0))
+            for i in range(nl - 1)
+        ]
 
     def place(buf, r, slots):
         for c in range(slots):
@@ -186,9 +200,13 @@
         place(lrbuf, r, lcap)
     for b in range(blocks):
         out_ref[pl.ds(b, comp, stride=blocks), :] = acc[b]
-    for r, copy in enumerate(tops, 1):
+    for copy in tops:
         copy.wait_recv()
-        row += urecv[r]
+    terms = [row] + [urecv[i] for i in range(len(tops))]
+    while len(terms) > 1:
+        half = len(terms) // 2
+        terms = [a + b for a, b in zip(terms[:half], terms[half:])] + terms[2 * half :]
+    row = terms[0]
     tot_ref[...] = (row / (cells * blocks))[0, :comp]
     for copy in sends:
         copy.wait_send()
@@ -197,6 +215,8 @@
 def solution(mesh):
     nd = mesh.shape["dev"]
     nl = mesh.shape["level"]
+    direct = nd * nl <= 64
+    last = (nd if direct else 1) * nl
 
     def body(
         fields,
@@ -220,7 +240,7 @@
         vmem = pl.BlockSpec(memory_space=pltpu.VMEM)
         dma = pltpu.SemaphoreType.DMA
         remapped, totals = pl.pallas_call(
-            functools.partial(kernel, nd, nl),
+            functools.partial(kernel, nd, nl, direct),
             out_shape=(
                 pltpu.VMEM((comp * blocks, cells), F32),
                 pltpu.VMEM((comp,), F32),
@@ -239,7 +259,7 @@
                 pltpu.VMEM((blocks, cells, cells), BF16),
                 pltpu.VMEM((nd, cap, cells, cells), BF16),
                 pltpu.VMEM((nl, lcap, cells, cells), BF16),
-                dma((11,)),
+                dma((9 + nd + nl,)),
                 pltpu.VMEM((nd, cap * rows, cells), BF16),
                 pltpu.VMEM((nd, cap * rows, cells), BF16),
                 dma((nd,)),
@@ -253,9 +273,9 @@
                 dma((nd,)),
                 dma((nd,)),
                 pltpu.VMEM((1, cells), F32),
-                pltpu.VMEM((nl, 1, cells), F32),
-                dma((nl,)),
-                dma((nl,)),
+                pltpu.VMEM((last, 1, cells), F32),
+                dma((last,)),
+                dma((last,)),
             ],
             compiler_params=pltpu.CompilerParams(collective_id=0, has_side_effects=True),
         )(

time: 15 us -> 13.6 us (0.907)
  Pallas kernels: 13.1 us -> 11.7 us
    pallas_call x1, Pallas kernels: 13.1 us -> 11.7 us  [body(): pl.pallas_call(functools.partial(kernel, nd, nl, direct), out_shape=(pltp...]
where the time goes in v3:
time: 13.6 us; the launch traced here: 13.5 us
  Pallas kernels  11.7 us (86%)
  local copies, waits for them, and re-layouts  1.15 us (8%)
  between operations  0.64 us (5%)
    pallas_call x1, Pallas kernels, body(): pl.pallas_call(functools.partial(kernel, nd, nl, direct), out_shape=(pltp...  11.7 us
    unnamed x2, local copies, waits for them, and re-layouts  1.15 us

profile of v3, /device:TPU:0, one launch (start us, length us, event | category | flops | bytes accessed | tf_op | source)
XLA Modules:
  0.0 13.5 jit_solution(15967226087477003376)
XLA Ops:
  0.6 11.7 %shard_map.122 = (f32[192,128]{1,0:T(8,128)S(1)}, f32[12]{0:T(128)S(1)}) custom-call(s32[1,16]{1,0:T(1,128)} %own_src_hbm.1, s32[2,8]{1,0:T(2,128)} %bitcast.32, s32[2,8]{1,0:T(2,128)} %bitcast.33, s32[1,8]{1,0:T(1,128)} %bitcast.36, s32[2,4]{1,0:T(2,128)} %bitcast.34, s32[2,4]{1,0:T(2,128)} %bitcast.35, s32[1,4]{1,0:T(1,128)} %bitcast.37, ...), custom_call_target="tpu_custom_call" | custom-call | tf_op jit(solution)/shard_map/pallas_call | solution.py:242
  12.3 0.6 %copy.15 = f32[1,16,12,128]{3,1,2,0:T(8,128)} copy(f32[1,16,12,128]{3,1,2,0:T(8,128)S(1)} %bitcast.27) | data formatting | bytes 196608
  13.0 0.5 %copy.16 = f32[12]{0:T(128)} copy(f32[12]{0:T(128)S(1)} %get-tuple-element.7) | data formatting | bytes 96

commit v4 on v3

--- a/solution.py
+++ b/solution.py
@@ -67,18 +67,6 @@
     rows = sbuf.shape[1] // cap
 
     barrier = pltpu.get_barrier_semaphore()
-    def peer_of(l, r):
-        return {"level": lax.rem(lvl + l, nl), "dev": lax.rem(dev + r, nd)}
-
-    offsets = [
-        (l, r)
-        for l in range(nl)
-        for r in range(nd)
-        if (l or r) and (direct or not (l and r))
-    ]
-    for l, r in offsets:
-        pl.semaphore_signal(barrier, inc=1, device_id=peer_of(l, r), device_id_type=MESH)
-
     left_peers = [lax.rem(lvl + r, nl) for r in range(1, nl)]
     send_peers = [lax.rem(dev + r, nd) for r in range(1, nd)]
     pairs = (
@@ -100,6 +88,18 @@
     for load in loads:
         load.start()
 
+    def peer_of(l, r):
+        return {"level": lax.rem(lvl + l, nl), "dev": lax.rem(dev + r, nd)}
+
+    offsets = [
+        (l, r)
+        for l in reversed(range(nl))
+        for r in reversed(range(nd))
+        if (l or r) and (direct or not (l and r))
+    ]
+    for l, r in offsets:
+        pl.semaphore_signal(barrier, inc=1, device_id=peer_of(l, r), device_id_type=MESH)
+
     part = jnp.zeros((comp, cells), F32)
 
     def donor(index):
@@ -131,6 +131,21 @@
         for c in range(cap):
             part += message(sbuf, r, c, send_block, send_target, send_count, send_w, peer)
 
+    for load in loads[second:]:
+        load.wait()
+    acc = []
+    for b in range(blocks):
+        term = product(donor(own_src[0, b]), own_w[b])
+        part += term
+        acc.append(term)
+
+    sums = jnp.sum(part, axis=1, keepdims=True)
+    same = lax.broadcasted_iota(jnp.int32, (comp, cells), 0) == lax.broadcasted_iota(
+        jnp.int32, (comp, cells), 1
+    )
+    row = jnp.sum(jnp.where(same, sums, 0.0), axis=0, keepdims=True)
+    tbuf[...] = row
+
     pl.semaphore_wait(barrier, len(offsets))
 
     sends = []
@@ -143,28 +158,6 @@
         sends.append(copy)
         return copy
 
-    lefts = [
-        send(lsbuf.at[r], lrbuf.at[r], ls_sem.at[r], lr_sem.at[r], peer_of(r, 0))
-        for r in range(1, nl)
-    ]
-    intras = [
-        send(sbuf.at[r], rbuf.at[r], s_sem.at[r], r_sem.at[r], peer_of(0, r)) for r in range(1, nd)
-    ]
-
-    for load in loads[second:]:
-        load.wait()
-    acc = []
-    for b in range(blocks):
-        term = product(donor(own_src[0, b]), own_w[b])
-        part += term
-        acc.append(term)
-
-    sums = jnp.sum(part, axis=1, keepdims=True)
-    same = lax.broadcasted_iota(jnp.int32, (comp, cells), 0) == lax.broadcasted_iota(
-        jnp.int32, (comp, cells), 1
-    )
-    row = jnp.sum(jnp.where(same, sums, 0.0), axis=0, keepdims=True)
-    tbuf[...] = row
     if direct:
         tops = [
             send(tbuf, urecv.at[i], us_sem.at[i], ur_sem.at[i], peer_of(l, r))
@@ -175,6 +168,14 @@
             send(tbuf, trecv.at[r], ts_sem.at[r], tr_sem.at[r], peer_of(0, r))
             for r in range(1, nd)
         ]
+    lefts = [
+        send(lsbuf.at[r], lrbuf.at[r], ls_sem.at[r], lr_sem.at[r], peer_of(r, 0))
+        for r in range(1, nl)
+    ]
+    intras = [
+        send(sbuf.at[r], rbuf.at[r], s_sem.at[r], r_sem.at[r], peer_of(0, r)) for r in range(1, nd)
+    ]
+    if not direct:
         for r, copy in enumerate(tots, 1):
             copy.wait_recv()
             row += trecv[r]
@@ -200,6 +201,8 @@
         place(lrbuf, r, lcap)
     for b in range(blocks):
         out_ref[pl.ds(b, comp, stride=blocks), :] = acc[b]
+    for copy in sends:
+        copy.wait_send()
     for copy in tops:
         copy.wait_recv()
     terms = [row] + [urecv[i] for i in range(len(tops))]
@@ -208,8 +211,6 @@
         terms = [a + b for a, b in zip(terms[:half], terms[half:])] + terms[2 * half :]
     row = terms[0]
     tot_ref[...] = (row / (cells * blocks))[0, :comp]
-    for copy in sends:
-        copy.wait_send()
 
 
 def solution(mesh):

time: 13.6 us -> 13.5 us (level)
  Pallas kernels: 11.7 us -> 11.5 us
    pallas_call x1, Pallas kernels: 11.7 us -> 11.5 us  [body(): pl.pallas_call(functools.partial(kernel, nd, nl, direct), out_shape=(pltp...]
where the time goes in v4:
time: 13.5 us; the launch traced here: 13.3 us
  Pallas kernels  11.5 us (85%)
  local copies, waits for them, and re-layouts  1.15 us (9%)
  between operations  0.64 us (5%)
    pallas_call x1, Pallas kernels, body(): pl.pallas_call(functools.partial(kernel, nd, nl, direct), out_shape=(pltp...  11.5 us
    unnamed x2, local copies, waits for them, and re-layouts  1.15 us

profile of v4, /device:TPU:0, one launch (start us, length us, event | category | flops | bytes accessed | tf_op | source)
XLA Modules:
  0.0 13.3 jit_solution(9197234395047676893)
XLA Ops:
  0.6 11.5 %shard_map.122 = (f32[192,128]{1,0:T(8,128)S(1)}, f32[12]{0:T(128)S(1)}) custom-call(s32[1,16]{1,0:T(1,128)} %own_src_hbm.1, s32[2,8]{1,0:T(2,128)} %bitcast.32, s32[2,8]{1,0:T(2,128)} %bitcast.33, s32[1,8]{1,0:T(1,128)} %bitcast.36, s32[2,4]{1,0:T(2,128)} %bitcast.34, s32[2,4]{1,0:T(2,128)} %bitcast.35, s32[1,4]{1,0:T(1,128)} %bitcast.37, ...), custom_call_target="tpu_custom_call" | custom-call | tf_op jit(solution)/shard_map/pallas_call | solution.py:243
  12.2 0.6 %copy.15 = f32[1,16,12,128]{3,1,2,0:T(8,128)} copy(f32[1,16,12,128]{3,1,2,0:T(8,128)S(1)} %bitcast.27) | data formatting | bytes 196608
  12.8 0.5 %copy.16 = f32[12]{0:T(128)} copy(f32[12]{0:T(128)S(1)} %get-tuple-element.7) | data formatting | bytes 96

commit v5 on v4

--- a/solution.py
+++ b/solution.py
@@ -57,6 +57,7 @@
     urecv,
     us_sem,
     ur_sem,
+    entered,
 ):
     dev = lax.axis_index("dev")
     lvl = lax.axis_index("level")
@@ -97,7 +98,8 @@
         for r in reversed(range(nd))
         if (l or r) and (direct or not (l and r))
     ]
-    for l, r in offsets:
+    near = [(l, r) for l, r in offsets if not (l and r)]
+    for l, r in near:
         pl.semaphore_signal(barrier, inc=1, device_id=peer_of(l, r), device_id_type=MESH)
 
     part = jnp.zeros((comp, cells), F32)
@@ -131,6 +133,25 @@
         for c in range(cap):
             part += message(sbuf, r, c, send_block, send_target, send_count, send_w, peer)
 
+    pl.semaphore_wait(barrier, len(near))
+    if direct:
+        for l in reversed(range(1, nl)):
+            pl.semaphore_signal(entered, inc=1, device_id=peer_of(l, 0), device_id_type=MESH)
+
+    sends = []
+
+    def send(src, dst, s, d, who):
+        copy = pltpu.make_async_remote_copy(
+            src_ref=src, dst_ref=dst, send_sem=s, recv_sem=d, device_id=who, device_id_type=MESH
+        )
+        copy.start()
+        sends.append(copy)
+        return copy
+
+    intras = [
+        send(sbuf.at[r], rbuf.at[r], s_sem.at[r], r_sem.at[r], peer_of(0, r)) for r in range(1, nd)
+    ]
+
     for load in loads[second:]:
         load.wait()
     acc = []
@@ -146,19 +167,8 @@
     row = jnp.sum(jnp.where(same, sums, 0.0), axis=0, keepdims=True)
     tbuf[...] = row
 
-    pl.semaphore_wait(barrier, len(offsets))
-
-    sends = []
-
-    def send(src, dst, s, d, who):
-        copy = pltpu.make_async_remote_copy(
-            src_ref=src, dst_ref=dst, send_sem=s, recv_sem=d, device_id=who, device_id_type=MESH
-        )
-        copy.start()
-        sends.append(copy)
-        return copy
-
     if direct:
+        pl.semaphore_wait(entered, nl - 1)
         tops = [
             send(tbuf, urecv.at[i], us_sem.at[i], ur_sem.at[i], peer_of(l, r))
             for i, (l, r) in enumerate(offsets)
@@ -171,9 +181,6 @@
     lefts = [
         send(lsbuf.at[r], lrbuf.at[r], ls_sem.at[r], lr_sem.at[r], peer_of(r, 0))
         for r in range(1, nl)
-    ]
-    intras = [
-        send(sbuf.at[r], rbuf.at[r], s_sem.at[r], r_sem.at[r], peer_of(0, r)) for r in range(1, nd)
     ]
     if not direct:
         for r, copy in enumerate(tots, 1):
@@ -277,6 +284,7 @@
                 pltpu.VMEM((last, 1, cells), F32),
                 dma((last,)),
                 dma((last,)),
+                pltpu.SemaphoreType.REGULAR,
             ],
             compiler_params=pltpu.CompilerParams(collective_id=0, has_side_effects=True),
         )(

time: 13.5 us -> 15.6 us (1.16)
  Pallas kernels: 11.5 us -> 13.7 us
    pallas_call x1, Pallas kernels: 11.5 us -> 13.7 us  [body(): pl.pallas_call(functools.partial(kernel, nd, nl, direct), out_shape=(pltp...]
where the time goes in v5:
time: 15.6 us; the launch traced here: 15.5 us
  Pallas kernels  13.7 us (88%)
  local copies, waits for them, and re-layouts  1.15 us (7%)
  between operations  0.64 us (4%)
    pallas_call x1, Pallas kernels, body(): pl.pallas_call(functools.partial(kernel, nd, nl, direct), out_shape=(pltp...  13.7 us
    unnamed x2, local copies, waits for them, and re-layouts  1.15 us

profile of v5, /device:TPU:0, one launch (start us, length us, event | category | flops | bytes accessed | tf_op | source)
XLA Modules:
  0.0 15.5 jit_solution(5604544382013325865)
XLA Ops:
  0.6 13.7 %shard_map.122 = (f32[192,128]{1,0:T(8,128)S(1)}, f32[12]{0:T(128)S(1)}) custom-call(s32[1,16]{1,0:T(1,128)} %own_src_hbm.1, s32[2,8]{1,0:T(2,128)} %bitcast.32, s32[2,8]{1,0:T(2,128)} %bitcast.33, s32[1,8]{1,0:T(1,128)} %bitcast.36, s32[2,4]{1,0:T(2,128)} %bitcast.34, s32[2,4]{1,0:T(2,128)} %bitcast.35, s32[1,4]{1,0:T(1,128)} %bitcast.37, ...), custom_call_target="tpu_custom_call" | custom-call | tf_op jit(solution)/shard_map/pallas_call | solution.py:250
  14.3 0.6 %copy.15 = f32[1,16,12,128]{3,1,2,0:T(8,128)} copy(f32[1,16,12,128]{3,1,2,0:T(8,128)S(1)} %bitcast.27) | data formatting | bytes 196608
  14.9 0.5 %copy.16 = f32[12]{0:T(128)} copy(f32[12]{0:T(128)S(1)} %get-tuple-element.7) | data formatting | bytes 96

commit v6 on v4

--- a/solution.py
+++ b/solution.py
@@ -158,6 +158,9 @@
         sends.append(copy)
         return copy
 
+    intras = [
+        send(sbuf.at[r], rbuf.at[r], s_sem.at[r], r_sem.at[r], peer_of(0, r)) for r in range(1, nd)
+    ]
     if direct:
         tops = [
             send(tbuf, urecv.at[i], us_sem.at[i], ur_sem.at[i], peer_of(l, r))
@@ -171,9 +174,6 @@
     lefts = [
         send(lsbuf.at[r], lrbuf.at[r], ls_sem.at[r], lr_sem.at[r], peer_of(r, 0))
         for r in range(1, nl)
-    ]
-    intras = [
-        send(sbuf.at[r], rbuf.at[r], s_sem.at[r], r_sem.at[r], peer_of(0, r)) for r in range(1, nd)
     ]
     if not direct:
         for r, copy in enumerate(tots, 1):

time: 13.5 us -> 13.5 us (level)
  no operation moved by 1% of the time
where the time goes in v6:
time: 13.5 us; the launch traced here: 13.3 us
  Pallas kernels  11.5 us (85%)
  local copies, waits for them, and re-layouts  1.15 us (9%)
  between operations  0.64 us (5%)
    pallas_call x1, Pallas kernels, body(): pl.pallas_call(functools.partial(kernel, nd, nl, direct), out_shape=(pltp...  11.5 us
    unnamed x2, local copies, waits for them, and re-layouts  1.15 us

profile of v6, /device:TPU:0, one launch (start us, length us, event | category | flops | bytes accessed | tf_op | source)
XLA Modules:
  0.0 13.3 jit_solution(118514338425595433)
XLA Ops:
  0.6 11.5 %shard_map.122 = (f32[192,128]{1,0:T(8,128)S(1)}, f32[12]{0:T(128)S(1)}) custom-call(s32[1,16]{1,0:T(1,128)} %own_src_hbm.1, s32[2,8]{1,0:T(2,128)} %bitcast.32, s32[2,8]{1,0:T(2,128)} %bitcast.33, s32[1,8]{1,0:T(1,128)} %bitcast.36, s32[2,4]{1,0:T(2,128)} %bitcast.34, s32[2,4]{1,0:T(2,128)} %bitcast.35, s32[1,4]{1,0:T(1,128)} %bitcast.37, ...), custom_call_target="tpu_custom_call" | custom-call | tf_op jit(solution)/shard_map/pallas_call | solution.py:243
  12.2 0.6 %copy.15 = f32[1,16,12,128]{3,1,2,0:T(8,128)} copy(f32[1,16,12,128]{3,1,2,0:T(8,128)S(1)} %bitcast.27) | data formatting | bytes 196608
  12.8 0.5 %copy.16 = f32[12]{0:T(128)} copy(f32[12]{0:T(128)S(1)} %get-tuple-element.7) | data formatting | bytes 96
